TPU v7x, 32 devices: a whole 2x2x4 slice. The times are simulated.
32 devices in a mesh: facet: 4 (over z), chan: 8 (over y, x, core).
Axes of the slice: x: 2, y: 2, z: 4, core: 2. Of those that a mesh axis runs over, the one named last changes fastest.
Arguments:
- visibilities: bfloat16 [2, 8, 256, 32, 128], P(None, None, None, ('facet', 'chan')), may hold values from -12 to 12
- kernels: bfloat16 [32, 256, 512], replicated, may hold values from -0.25 to 0.25
- delays: float32 [8, 256, 128], P('facet'), may hold values from -4 to 4
- tile_of: int32 [8, 256], P('facet'), may hold values from 0 to 127
- plane_of: int32 [8, 256], P('facet'), may hold values from 0 to 31
- counts: int32 [8], P('facet'), may hold values from 64 to 256
- neighbours: int32 [8, 4], replicated, may hold values from 0 to 7, as said below
Outputs:
- joined_grids: float32 [128, 8, 4, 512], P('chan', 'facet')
Inputs may be any that keep to these rules, and one draw needn't show every extreme that they name: `neighbours`: each row names 4 different facets, none of them its own.
All inputs are finite; a program needn't handle non-finite values.
Results may differ from a plain program's by a relative error of at most 0.0043.
Values may be sent and summed in bfloat16 or wider, within the bound.
A program may use at most 128 MiB of HBM per device.

v0:
```python
import functools
import math

import jax
import jax.numpy as jnp
from jax import lax
from jax.experimental import pallas as pl
from jax.experimental.pallas import tpu as pltpu
from jax.sharding import PartitionSpec as P

AVG = 8
TS = 16
NT_DEV = 16
EDGE = 4
LANES = 128
MESH = pl.DeviceIdType.MESH


def series(first, count, scale):
    return [
        (-1.0) ** i * scale ** (2 * i + first) / math.factorial(2 * i + first)
        for i in range(count)
    ]


SIN_HALF = series(1, 7, math.pi)
COS_HALF = series(0, 7, math.pi)


def turn_parts(turns):
    frac = turns - jnp.round(turns)
    square = frac * frac
    sine = jnp.full_like(frac, SIN_HALF[-1])
    cosine = jnp.full_like(frac, COS_HALF[-1])
    for a, b in zip(SIN_HALF[-2::-1], COS_HALF[-2::-1]):
        sine = sine * square + a
        cosine = cosine * square + b
    sine = sine * frac
    return 1.0 - 2.0 * sine * sine, 2.0 * sine * cosine


def kernel(
    cfg,
    neigh_ref,
    vis_ref,
    delay_ref,
    code_ref,
    kern_ref,
    out_ref,
    got,
    turns,
    codes,
    rows,
    kern,
    lhs,
    grid,
    final,
    vis_send,
    vis_recv,
    turn_send,
    turn_recv,
    code_send,
    code_recv,
    row_send,
    row_recv,
    relay_send,
    relay_recv,
    fin_send,
    fin_recv,
    own_sem,
    kern_sem,
):
    n, nz, facets, fac, blk, groups, planes, tiles, chunks = cfg
    me = lax.axis_index("chan")
    zme = lax.axis_index("facet")
    channels = groups * AVG * nz
    cells = kern_ref.shape[1]
    tile = cells // 2
    edge = EDGE * TS
    per = facets // chunks
    pairs = n // 2
    mate = me + 1 - 2 * lax.rem(me, 2)
    parity = lax.rem(me, 2)
    my_pair = me // 2

    load_kern = pltpu.make_async_copy(kern_ref, kern, kern_sem)
    load_kern.start()

    barrier = pltpu.get_barrier_semaphore()
    for d in range(1, n):
        pl.semaphore_signal(
            barrier, inc=1, device_id={"chan": lax.rem(me + d, n)}, device_id_type=MESH
        )
    for d in range(1, nz):
        pl.semaphore_signal(
            barrier, inc=1, device_id={"facet": lax.rem(zme + d, nz)}, device_id_type=MESH
        )

    my_blocks = pl.ds(pl.multiple_of(me * blk, blk), blk)
    my_facets = pl.ds(zme * fac, fac)

    def own_copy(c):
        return pltpu.make_async_copy(
            vis_ref.at[:, pl.ds(c * per, per), my_blocks],
            got.at[me, :, pl.ds(c * per, per)],
            own_sem.at[c],
        )

    own_turns = pltpu.make_async_copy(
        delay_ref.at[:, my_blocks], turns.at[my_facets], own_sem.at[chunks]
    )
    own_codes = pltpu.make_async_copy(code_ref, codes.at[my_facets], own_sem.at[chunks + 1])
    for c in range(chunks):
        own_copy(c).start()
    own_turns.start()
    own_codes.start()
    pl.semaphore_wait(barrier, n + nz - 2)

    def vis_copy(peer, slot, c, d):
        return pltpu.make_async_remote_copy(
            src_ref=vis_ref.at[:, pl.ds(c * per, per), pl.ds(pl.multiple_of(peer * blk, blk), blk)],
            dst_ref=got.at[slot, :, pl.ds(c * per, per)],
            send_sem=vis_send.at[d, c],
            recv_sem=vis_recv.at[d, c],
            device_id={"chan": peer},
            device_id_type=MESH,
        )

    def turn_copy(peer, slot, d):
        return pltpu.make_async_remote_copy(
            src_ref=delay_ref.at[:, my_blocks],
            dst_ref=turns.at[pl.ds(slot * fac, fac)],
            send_sem=turn_send.at[d],
            recv_sem=turn_recv.at[d],
            device_id={"facet": peer},
            device_id_type=MESH,
        )

    def code_copy(peer, slot, d):
        return pltpu.make_async_remote_copy(
            src_ref=code_ref,
            dst_ref=codes.at[pl.ds(slot * fac, fac)],
            send_sem=code_send.at[d],
            recv_sem=code_recv.at[d],
            device_id={"facet": peer},
            device_id_type=MESH,
        )

    for d in range(1, nz):
        turn_copy(lax.rem(zme + d, nz), zme, d).start()
    for c in range(chunks):
        for d in range(1, n):
            vis_copy(lax.rem(me + d, n), me, c, d).start()
    for d in range(1, nz):
        code_copy(lax.rem(zme + d, nz), zme, d).start()

    def row_copy(owner, peer, c, send, recv):
        part = rows.at[
            pl.ds(c * per, per), pl.ds(pl.multiple_of(owner * blk, blk), blk)
        ]
        return pltpu.make_async_remote_copy(
            src_ref=part,
            dst_ref=part,
            send_sem=send,
            recv_sem=recv,
            device_id={"chan": peer},
            device_id_type=MESH,
        )

    own_turns.wait()
    for d in range(1, nz):
        turn_copy(lax.rem(zme + d, nz), lax.rem(zme + nz - d, nz), d).wait_recv()

    for c in range(chunks):
        own_copy(c).wait()
        for d in range(1, n):
            vis_copy(lax.rem(me + d, n), lax.rem(me + n - d, n), c, d).wait_recv()

        def rotate(i, carry):
            f = c * per + i
            delay = turns[f]
            step_cos, step_sin = turn_parts(delay * (0.5 / channels))
            for g in range(groups):
                first = (zme * groups + g) * AVG
                start_cos, start_sin = turn_parts(
                    delay * (1.0 + (0.5 / channels) * first.astype(jnp.float32))
                )
                real = got[g * AVG + AVG - 1, 0, f].astype(jnp.float32)
                imag = got[g * AVG + AVG - 1, 1, f].astype(jnp.float32)
                for k in range(AVG - 2, -1, -1):
                    next_real = got[g * AVG + k, 0, f].astype(jnp.float32) + (
                        real * step_cos - imag * step_sin
                    )
                    imag = got[g * AVG + k, 1, f].astype(jnp.float32) + (
                        real * step_sin + imag * step_cos
                    )
                    real = next_real
                rows[f, my_blocks, 2 * LANES * g : 2 * LANES * g + LANES] = (
                    (real * start_cos - imag * start_sin) * (1.0 / AVG)
                ).astype(jnp.bfloat16)
                rows[f, my_blocks, 2 * LANES * g + LANES : 2 * LANES * (g + 1)] = (
                    (real * start_sin + imag * start_cos) * (1.0 / AVG)
                ).astype(jnp.bfloat16)
            return carry

        lax.fori_loop(0, per, rotate, 0)
        for q in range(1, pairs):
            peer = 2 * lax.rem(my_pair + q, pairs) + parity
            row_copy(me, peer, c, row_send.at[q, c], row_recv.at[q, c]).start()
        row_copy(me, mate, c, row_send.at[0, c], row_recv.at[0, c]).start()

    own_codes.wait()
    for d in range(1, nz):
        code_copy(lax.rem(zme + d, nz), lax.rem(zme + nz - d, nz), d).wait_recv()

    for c in range(chunks):
        for q in range(1, pairs):
            owner = 2 * lax.rem(my_pair + pairs - q, pairs) + parity
            row_copy(owner, mate, c, row_send.at[q, c], row_recv.at[q, c]).wait_recv()
            row_copy(owner, mate, c, relay_send.at[q, c], relay_recv.at[q, c]).start()

    entry = lax.broadcasted_iota(jnp.int32, (planes * NT_DEV, blk * n), 0)
    wanted = (entry // NT_DEV) * tiles + me * NT_DEV + lax.rem(entry, NT_DEV)
    for c in range(chunks):
        row_copy(mate, mate, c, row_send.at[0, c], row_recv.at[0, c]).wait_recv()
        for q in range(1, pairs):
            owner = 2 * lax.rem(my_pair + pairs - q, pairs) + 1 - parity
            row_copy(owner, mate, c, relay_send.at[q, c], relay_recv.at[q, c]).wait_recv()

        for i in range(per):
            f = c * per + i
            table = (codes[f] == wanted).astype(jnp.float32).astype(jnp.bfloat16)
            summed = jnp.dot(table, rows[f], preferred_element_type=jnp.float32).astype(
                jnp.bfloat16
            )
            for g in range(groups):
                at = (g * facets + f) * NT_DEV
                for p in range(planes):
                    lhs[at : at + NT_DEV, 2 * LANES * p : 2 * LANES * (p + 1)] = summed[
                        p * NT_DEV : (p + 1) * NT_DEV, 2 * LANES * g : 2 * LANES * (g + 1)
                    ]

    load_kern.wait()
    grid[...] = jnp.dot(lhs[...], kern[...], preferred_element_type=jnp.float32)

    span = facets * NT_DEV
    row_id = lax.broadcasted_iota(jnp.int32, (NT_DEV, span), 0)
    col_id = lax.broadcasted_iota(jnp.int32, (NT_DEV, span), 1)
    same_tile = lax.rem(col_id, NT_DEV) == row_id
    col_facet = col_id // NT_DEV
    parts = []
    for f in range(facets):
        weight = jnp.zeros((NT_DEV, span), jnp.float32)
        for k in range(neigh_ref.shape[1]):
            weight += jnp.where(same_tile & (col_facet == neigh_ref[f, k]), 0.25, 0.0)
        parts.append(weight)
    mix = jnp.concatenate(parts, axis=0).astype(jnp.bfloat16)
    keep = lax.broadcasted_iota(jnp.int32, (span, LANES), 1) >= LANES - edge
    for g in range(groups):
        here = slice(g * span, (g + 1) * span)
        for half in range(2):
            base = half * tile
            strip = grid[here, base : base + LANES].astype(jnp.bfloat16)
            blended = jnp.dot(mix, strip, preferred_element_type=jnp.float32)
            moved = pltpu.roll(blended, LANES - edge, 1)
            last = slice(base + tile - LANES, base + tile)
            grid[here, last] += jnp.where(keep, moved, 0.0)
    for z in range(nz):
        for g in range(groups):
            at = (g * facets + z * fac) * NT_DEV
            final[z, g] = grid[at : at + fac * NT_DEV].astype(jnp.bfloat16)

    def fin_copy(peer, slot, d):
        return pltpu.make_async_remote_copy(
            src_ref=final.at[peer],
            dst_ref=out_ref.at[slot],
            send_sem=fin_send.at[d],
            recv_sem=fin_recv.at[d],
            device_id={"facet": peer},
            device_id_type=MESH,
        )

    for d in range(1, nz):
        fin_copy(lax.rem(zme + d, nz), zme, d).start()
    out_ref[zme] = final[zme]

    for d in range(1, nz):
        turn_copy(lax.rem(zme + d, nz), zme, d).wait_send()
        code_copy(lax.rem(zme + d, nz), zme, d).wait_send()
    for c in range(chunks):
        for d in range(1, n):
            vis_copy(lax.rem(me + d, n), me, c, d).wait_send()
        for q in range(pairs):
            row_copy(me, mate, c, row_send.at[q, c], row_recv.at[q, c]).wait_send()
        for q in range(1, pairs):
            row_copy(me, mate, c, relay_send.at[q, c], relay_recv.at[q, c]).wait_send()
    for d in range(1, nz):
        fin_copy(lax.rem(zme + d, nz), zme, d).wait_send()
        fin_copy(lax.rem(zme + d, nz), lax.rem(zme + nz - d, nz), d).wait_recv()


CHUNKS = 2


def local(visibilities, kernels, delays, tile_of, plane_of, counts, neighbours):
    n = lax.axis_size("chan")
    nz = lax.axis_size("facet")
    halves, facets, blocks, ch_dev, lanes = visibilities.shape
    planes, depth, cells = kernels.shape
    fac = facets // nz
    blk = blocks // n
    groups = n * ch_dev // AVG
    tiles = NT_DEV * n
    chunks = CHUNKS
    vis = visibilities.reshape(halves, facets, blocks, lanes)
    block_id = jnp.arange(blocks, dtype=jnp.int32)[None, :]
    code = jnp.where(block_id < counts[:, None], plane_of * tiles + tile_of, -1)
    code = code.reshape(fac, 1, blocks)
    cfg = (n, nz, facets, fac, blk, groups, planes, tiles, chunks)
    dma = pltpu.SemaphoreType.DMA
    span = facets * NT_DEV
    out = pl.pallas_call(
        functools.partial(kernel, cfg),
        out_shape=jax.ShapeDtypeStruct((nz, groups, fac * NT_DEV, cells), jnp.bfloat16),
        in_specs=[
            pl.BlockSpec(memory_space=pltpu.SMEM),
            pl.BlockSpec(memory_space=pl.ANY),
            pl.BlockSpec(memory_space=pl.ANY),
            pl.BlockSpec(memory_space=pltpu.VMEM),
            pl.BlockSpec(memory_space=pl.ANY),
        ],
        out_specs=pl.BlockSpec(memory_space=pltpu.VMEM),
        scratch_shapes=[
            pltpu.VMEM((n, halves, facets, blk, lanes), jnp.bfloat16),
            pltpu.VMEM((facets, blk, lanes), jnp.float32),
            pltpu.VMEM((facets, 1, blocks), jnp.int32),
            pltpu.VMEM((facets, blocks, groups * depth), jnp.bfloat16),
            pltpu.VMEM((planes * depth, cells), jnp.bfloat16),
            pltpu.VMEM((groups * span, planes * depth), jnp.bfloat16),
            pltpu.VMEM((groups * span, cells), jnp.float32),
            pltpu.VMEM((nz, groups, fac * NT_DEV, cells), jnp.bfloat16),
            dma((n, chunks)),
            dma((n, chunks)),
            dma((nz,)),
            dma((nz,)),
            dma((nz,)),
            dma((nz,)),
            dma((n // 2, chunks)),
            dma((n // 2, chunks)),
            dma((n // 2, chunks)),
            dma((n // 2, chunks)),
            dma((nz,)),
            dma((nz,)),
            dma((chunks + 2,)),
            dma,
        ],
        compiler_params=pltpu.CompilerParams(
            collective_id=0, has_side_effects=True, vmem_limit_bytes=60 * 1024 * 1024
        ),
    )(neighbours, vis, delays, code, kernels.reshape(planes * depth, cells))
    spread = out.reshape(nz * groups, fac, NT_DEV, cells).astype(jnp.float32)
    return jnp.transpose(spread, (2, 1, 0, 3))


def solution(mesh):
    return jax.shard_map(
        local,
        mesh=mesh,
        in_specs=(
            P(None, None, None, ("facet", "chan"), None),
            P(),
            P("facet", None, None),
            P("facet", None),
            P("facet", None),
            P("facet"),
            P(),
        ),
        out_specs=P("chan", "facet", None, None),
        check_vma=False,
    )
```

profile of v0, /device:TPU:0, one launch (start us, length us, event | category | flops | bytes accessed | tf_op | source)
XLA Modules:
  0.0 37.8 jit_solution(17979833027447391399)
XLA Ops:
  0.0 0.8 %compare_select_fusion = s32[2,256]{1,0:T(2,128)S(1)} fusion(s32[2,256]{1,0:T(2,128)} %param.10, s32[2,256]{1,0:T(2,128)} %param.11, s32[2]{0:T(128)} %param.12), kind=kLoop, calls=%fused_computation.1 | loop fusion | flops 2048 | bytes 6152 | tf_op jit(solution)/shard_map/jit(_where)/select_n | solution.py:317
  0.8 0.6 %reshape.14.code_ref = s32[2,1,256]{2,1,0:T(1,128)} reshape(s32[2,256]{1,0:T(2,128)S(1)} %compare_select_fusion) | data formatting | bytes 4096 | tf_op jit(solution)/shard_map/reshape | solution.py:318
  1.4 1.3 %copy.8.neigh_ref = s32[8,4]{1,0:T(8,128)} copy(s32[8,4]{0,1:T(4,128)} %param.13) | data formatting | bytes 256 | tf_op args[6]
  2.7 33.4 %shard_map.73 = bf16[4,1,32,512]{3,2,1,0:T(8,128)(2,1)} custom-call(s32[8,4]{1,0:T(8,128)} %copy.8.neigh_ref, bf16[2,8,256,128]{3,2,1,0:T(8,128)(2,1)} %bitcast.8, f32[2,256,128]{2,1,0:T(8,128)} %delay_ref.1, s32[2,1,256]{2,1,0:T(1,128)} %reshape.14.code_ref, bf16[8192,512]{1,0:T(8,128)(2,1)} %bitcast.7), custom_call_target="tpu_custom_call" | custom-call | tf_op jit(solution)/shard_map/pallas_call | solution.py:322
  36.1 1.7 %copy.11 = f32[4,2,16,512]{3,0,1,2:T(4,128)} copy(bf16[4,2,16,512]{3,2,1,0:T(8,128)(2,1)} %bitcast.9) | data formatting | bytes 393216 | tf_op jit(solution)/shard_map/transpose | solution.py:362
where the time goes:
time: 38 us; the launch traced here: 37.8 us
  Pallas kernels  33.4 us (88%)
  local copies, waits for them, and re-layouts  3.65 us (10%)
  other arithmetic  0.77 us (2%)
    pallas_call x1, Pallas kernels, local(): pl.pallas_call(functools.partial(kernel, cfg), out_shape=jax.ShapeDtypeSt...  33.4 us
    transpose x1, local copies, waits for them, and re-layouts, local(): return jnp.transpose(spread, (2, 1, 0, 3))  1.71 us
    unnamed x1, local copies, waits for them, and re-layouts  1.35 us
    select_n x1, other arithmetic, local(): code = jnp.where(block_id < counts[:, None], plane_of * tiles + tile_of, -1)  0.77 us

commit v1 on v0

v1 whole, which is shorter than its diff:
```python
import functools
import math

import jax
import jax.numpy as jnp
from jax import lax
from jax.experimental import pallas as pl
from jax.experimental.pallas import tpu as pltpu
from jax.sharding import PartitionSpec as P

AVG = 8
TS = 16
NT_DEV = 16
EDGE = 4
LANES = 128
MESH = pl.DeviceIdType.MESH


def series(first, count, scale):
    return [
        (-1.0) ** i * scale ** (2 * i + first) / math.factorial(2 * i + first)
        for i in range(count)
    ]


SIN_HALF = series(1, 7, math.pi)
COS_HALF = series(0, 7, math.pi)


def turn_parts(turns):
    frac = turns - jnp.round(turns)
    square = frac * frac
    sine = jnp.full_like(frac, SIN_HALF[-1])
    cosine = jnp.full_like(frac, COS_HALF[-1])
    for a, b in zip(SIN_HALF[-2::-1], COS_HALF[-2::-1]):
        sine = sine * square + a
        cosine = cosine * square + b
    sine = sine * frac
    return 1.0 - 2.0 * sine * sine, 2.0 * sine * cosine


def flip(index, mask):
    bit = 1
    while bit <= mask:
        if mask & bit:
            index = index + bit - 2 * bit * lax.rem(index // bit, 2)
        bit *= 2
    return index


def kernel(
    cfg,
    neigh_ref,
    count_ref,
    vis_ref,
    delay_ref,
    tile_ref,
    plane_ref,
    kern_ref,
    out_ref,
    pair,
    part,
    got,
    wide,
    rough,
    turns,
    codes,
    rows,
    kern,
    lhs,
    grid,
    final,
    mate_send,
    mate_recv,
    rough_send,
    rough_recv,
    turn_send,
    turn_recv,
    code_send,
    code_recv,
    part_send,
    part_recv,
    row_send,
    row_recv,
    relay_send,
    relay_recv,
    fin_send,
    fin_recv,
    own_sem,
    kern_sem,
):
    n, nz, facets, fac, blk, groups, planes, tiles = cfg
    me = lax.axis_index("chan")
    zme = lax.axis_index("facet")
    channels = groups * AVG * nz
    tile = kern_ref.shape[1] // 2
    edge = EDGE * TS
    pairs = n // 2
    parity = lax.rem(me, 2)
    mate = me + 1 - 2 * parity
    my_pair = me // 2
    half_avg = AVG // 2
    chunk_z = [flip(zme, c) for c in range(nz)]

    def group_of(c):
        return pl.ds(chunk_z[c] * fac, fac)

    load_kern = pltpu.make_async_copy(kern_ref, kern, kern_sem)
    own_wide = pltpu.make_async_copy(delay_ref.at[:, :, parity], wide, own_sem.at[nz])
    own_turns = pltpu.make_async_copy(
        delay_ref.at[:, my_pair, parity], turns.at[zme], own_sem.at[nz + 1]
    )

    def own_copy(c):
        return pltpu.make_async_copy(
            vis_ref.at[:, group_of(c), :, parity],
            pair.at[parity, :, group_of(c)],
            own_sem.at[c],
        )

    barrier = pltpu.get_barrier_semaphore()
    for d in range(1, n):
        pl.semaphore_signal(
            barrier, inc=1, device_id={"chan": lax.rem(me + d, n)}, device_id_type=MESH
        )
    for d in range(1, nz):
        pl.semaphore_signal(
            barrier, inc=1, device_id={"facet": chunk_z[d]}, device_id_type=MESH
        )
    own_wide.start()
    for c in range(nz):
        own_copy(c).start()
    own_turns.start()
    load_kern.start()

    blocks = blk * n
    block_id = lax.broadcasted_iota(jnp.int32, (1, blocks), 1)
    for i in range(fac):
        codes[zme, i : i + 1] = jnp.where(
            block_id < count_ref[i],
            plane_ref[i : i + 1] * tiles + tile_ref[i : i + 1],
            -1,
        )
    own_wide.wait()
    rough[zme] = wide[...].astype(jnp.bfloat16)
    pl.semaphore_wait(barrier, n + nz - 2)

    def mate_copy(c, slot):
        return pltpu.make_async_remote_copy(
            src_ref=vis_ref.at[:, group_of(c), :, 1 - parity],
            dst_ref=pair.at[slot, :, group_of(c)],
            send_sem=mate_send.at[c],
            recv_sem=mate_recv.at[c],
            device_id={"chan": mate},
            device_id_type=MESH,
        )

    def facet_copy(src, buffer, slot, d, send, recv):
        return pltpu.make_async_remote_copy(
            src_ref=src,
            dst_ref=buffer.at[slot],
            send_sem=send.at[d],
            recv_sem=recv.at[d],
            device_id={"facet": chunk_z[d]},
            device_id_type=MESH,
        )

    def rough_copy(d, slot):
        return facet_copy(rough.at[zme], rough, slot, d, rough_send, rough_recv)

    def turn_copy(d, slot):
        return facet_copy(
            delay_ref.at[:, my_pair, parity], turns, slot, d, turn_send, turn_recv
        )

    def code_copy(d, slot):
        return facet_copy(codes.at[zme], codes, slot, d, code_send, code_recv)

    for c in range(nz):
        mate_copy(c, parity).start()
    for d in range(1, nz):
        turn_copy(d, zme).start()
    for d in range(1, nz):
        rough_copy(d, zme).start()
    for d in range(1, nz):
        code_copy(d, zme).start()

    my_blocks = pl.ds(pl.multiple_of(me * blk, blk), blk)

    def part_copy(c, d, owner, slot):
        return pltpu.make_async_remote_copy(
            src_ref=part.at[owner, :, group_of(c)],
            dst_ref=got.at[slot, :, group_of(c)],
            send_sem=part_send.at[d, c],
            recv_sem=part_recv.at[d, c],
            device_id={"chan": 2 * owner + parity},
            device_id_type=MESH,
        )

    def row_copy(owner, peer, c, send, recv):
        piece = rows.at[group_of(c), pl.ds(pl.multiple_of(owner * blk, blk), blk)]
        return pltpu.make_async_remote_copy(
            src_ref=piece,
            dst_ref=piece,
            send_sem=send,
            recv_sem=recv,
            device_id={"chan": peer},
            device_id_type=MESH,
        )

    def after(d):
        return lax.rem(my_pair + d, pairs)

    def before(d):
        return lax.rem(my_pair + pairs - d, pairs)

    def join_pair(c):
        own_copy(c).wait()
        mate_copy(c, 1 - parity).wait_recv()
        if c:
            rough_copy(c, chunk_z[c]).wait_recv()

        def one(i, carry):
            slot = i // pairs
            q = lax.rem(i, pairs)
            f = chunk_z[c] * fac + slot
            cosine, sine = turn_parts(
                rough[chunk_z[c], slot, q].astype(jnp.float32) * (0.5 / channels)
            )
            real = pair[1, 0, f, q].astype(jnp.float32)
            imag = pair[1, 1, f, q].astype(jnp.float32)
            part[q, 0, f] = (
                pair[0, 0, f, q].astype(jnp.float32) + (real * cosine - imag * sine)
            ).astype(jnp.bfloat16)
            part[q, 1, f] = (
                pair[0, 1, f, q].astype(jnp.float32) + (real * sine + imag * cosine)
            ).astype(jnp.bfloat16)
            return carry

        lax.fori_loop(0, fac * pairs, one, 0)
        for d in range(1, pairs):
            part_copy(c, d, after(d), my_pair).start()
        got[my_pair, :, group_of(c)] = part[my_pair, :, group_of(c)]

    def rotate(c):
        if c:
            turn_copy(c, chunk_z[c]).wait_recv()
        else:
            own_turns.wait()
        for d in range(1, pairs):
            part_copy(c, d, after(d), before(d)).wait_recv()

        def one(i, carry):
            f = chunk_z[c] * fac + i
            delay = turns[chunk_z[c], i]
            step_cos, step_sin = turn_parts(delay * (1.0 / channels))
            for g in range(groups):
                first = (zme * groups + g) * AVG
                start_cos, start_sin = turn_parts(
                    delay * (1.0 + (0.5 / channels) * first.astype(jnp.float32))
                )
                top = (g + 1) * half_avg - 1
                real = got[top, 0, f].astype(jnp.float32)
                imag = got[top, 1, f].astype(jnp.float32)
                for k in range(top - 1, g * half_avg - 1, -1):
                    next_real = got[k, 0, f].astype(jnp.float32) + (
                        real * step_cos - imag * step_sin
                    )
                    imag = got[k, 1, f].astype(jnp.float32) + (
                        real * step_sin + imag * step_cos
                    )
                    real = next_real
                rows[f, my_blocks, 2 * LANES * g : 2 * LANES * g + LANES] = (
                    (real * start_cos - imag * start_sin) * (1.0 / AVG)
                ).astype(jnp.bfloat16)
                rows[f, my_blocks, 2 * LANES * g + LANES : 2 * LANES * (g + 1)] = (
                    (real * start_sin + imag * start_cos) * (1.0 / AVG)
                ).astype(jnp.bfloat16)
            return carry

        lax.fori_loop(0, fac, one, 0)
        for q in range(1, pairs):
            row_copy(me, 2 * after(q) + parity, c, row_send.at[q, c], row_recv.at[q, c]).start()
        row_copy(me, mate, c, row_send.at[0, c], row_recv.at[0, c]).start()

    def relay(c):
        for q in range(1, pairs):
            owner = 2 * before(q) + parity
            row_copy(owner, mate, c, row_send.at[q, c], row_recv.at[q, c]).wait_recv()
            row_copy(owner, mate, c, relay_send.at[q, c], relay_recv.at[q, c]).start()

    entry = lax.broadcasted_iota(jnp.int32, (planes * NT_DEV, blocks), 0)
    wanted = (entry // NT_DEV) * tiles + me * NT_DEV + lax.rem(entry, NT_DEV)

    def gather_rows(c):
        if c:
            code_copy(c, chunk_z[c]).wait_recv()
        row_copy(mate, mate, c, row_send.at[0, c], row_recv.at[0, c]).wait_recv()
        for q in range(1, pairs):
            owner = 2 * before(q) + 1 - parity
            row_copy(owner, mate, c, relay_send.at[q, c], relay_recv.at[q, c]).wait_recv()
        for i in range(fac):
            f = chunk_z[c] * fac + i
            code = codes[chunk_z[c], i : i + 1]
            table = (code == wanted).astype(jnp.float32).astype(jnp.bfloat16)
            summed = jnp.dot(table, rows[f], preferred_element_type=jnp.float32).astype(
                jnp.bfloat16
            )
            for g in range(groups):
                at = pl.ds(pl.multiple_of((g * facets + f) * NT_DEV, NT_DEV), NT_DEV)
                for p in range(planes):
                    lhs[at, 2 * LANES * p : 2 * LANES * (p + 1)] = summed[
                        p * NT_DEV : (p + 1) * NT_DEV, 2 * LANES * g : 2 * LANES * (g + 1)
                    ]

    stages = (join_pair, rotate, relay, gather_rows)
    for step in range(nz + len(stages) - 1):
        for lag, stage in enumerate(stages):
            if 0 <= step - lag < nz:
                stage(step - lag)

    span = facets * NT_DEV
    row_id = lax.broadcasted_iota(jnp.int32, (NT_DEV, span), 0)
    col_id = lax.broadcasted_iota(jnp.int32, (NT_DEV, span), 1)
    same_tile = lax.rem(col_id, NT_DEV) == row_id
    col_facet = col_id // NT_DEV
    weights = []
    for f in range(facets):
        weight = jnp.zeros((NT_DEV, span), jnp.float32)
        for k in range(neigh_ref.shape[0]):
            weight += jnp.where(same_tile & (col_facet == neigh_ref[k, f]), 0.25, 0.0)
        weights.append(weight)
    mix = jnp.concatenate(weights, axis=0).astype(jnp.bfloat16)
    keep = lax.broadcasted_iota(jnp.int32, (span, LANES), 1) >= LANES - edge

    def fin_copy(half, d, slot):
        return pltpu.make_async_remote_copy(
            src_ref=final.at[half, chunk_z[d]],
            dst_ref=out_ref.at[slot, :, :, pl.ds(half * tile, tile)],
            send_sem=fin_send.at[d, half],
            recv_sem=fin_recv.at[d, half],
            device_id={"facet": chunk_z[d]},
            device_id_type=MESH,
        )

    load_kern.wait()
    for half in range(2):
        grid[...] = jnp.dot(
            lhs[...],
            kern[:, half * tile : (half + 1) * tile],
            preferred_element_type=jnp.float32,
        )
        for g in range(groups):
            here = slice(g * span, (g + 1) * span)
            blended = jnp.dot(
                mix, grid[here, :LANES].astype(jnp.bfloat16), preferred_element_type=jnp.float32
            )
            moved = pltpu.roll(blended, LANES - edge, 1)
            grid[here, tile - LANES :] += jnp.where(keep, moved, 0.0)
        for z in range(nz):
            for g in range(groups):
                at = (g * facets + z * fac) * NT_DEV
                final[half, z, g] = grid[at : at + fac * NT_DEV].astype(jnp.bfloat16)
        for d in range(1, nz):
            fin_copy(half, d, zme).start()
        out_ref[zme, :, :, half * tile : (half + 1) * tile] = final[half, zme]

    for c in range(nz):
        mate_copy(c, parity).wait_send()
        for q in range(pairs):
            row_copy(me, mate, c, row_send.at[q, c], row_recv.at[q, c]).wait_send()
        for q in range(1, pairs):
            part_copy(c, q, after(q), my_pair).wait_send()
            row_copy(me, mate, c, relay_send.at[q, c], relay_recv.at[q, c]).wait_send()
    for d in range(1, nz):
        turn_copy(d, zme).wait_send()
        rough_copy(d, zme).wait_send()
        code_copy(d, zme).wait_send()
    for half in range(2):
        for d in range(1, nz):
            fin_copy(half, d, zme).wait_send()
            fin_copy(half, d, chunk_z[d]).wait_recv()


def local(visibilities, kernels, delays, tile_of, plane_of, counts, neighbours):
    n = lax.axis_size("chan")
    nz = lax.axis_size("facet")
    halves, facets, blocks, ch_dev, lanes = visibilities.shape
    planes, depth, cells = kernels.shape
    fac = facets // nz
    blk = blocks // n
    pairs = n // 2
    groups = n * ch_dev // AVG
    tiles = NT_DEV * n
    vis = visibilities.reshape(halves, facets, pairs, 2, blk, lanes)
    cfg = (n, nz, facets, fac, blk, groups, planes, tiles)
    dma = pltpu.SemaphoreType.DMA
    span = facets * NT_DEV
    smem = pl.BlockSpec(memory_space=pltpu.SMEM)
    vmem = pl.BlockSpec(memory_space=pltpu.VMEM)
    anywhere = pl.BlockSpec(memory_space=pl.ANY)
    out = pl.pallas_call(
        functools.partial(kernel, cfg),
        out_shape=jax.ShapeDtypeStruct((nz, groups, fac * NT_DEV, cells), jnp.bfloat16),
        in_specs=[smem, smem, anywhere, anywhere, vmem, vmem, anywhere],
        out_specs=vmem,
        scratch_shapes=[
            pltpu.VMEM((2, halves, facets, pairs, blk, lanes), jnp.bfloat16),
            pltpu.VMEM((pairs, halves, facets, blk, lanes), jnp.bfloat16),
            pltpu.VMEM((pairs, halves, facets, blk, lanes), jnp.bfloat16),
            pltpu.VMEM((fac, pairs, blk, lanes), jnp.float32),
            pltpu.VMEM((nz, fac, pairs, blk, lanes), jnp.bfloat16),
            pltpu.VMEM((nz, fac, blk, lanes), jnp.float32),
            pltpu.VMEM((nz, fac, blocks), jnp.int32),
            pltpu.VMEM((facets, blocks, groups * depth), jnp.bfloat16),
            pltpu.VMEM((planes * depth, cells), jnp.bfloat16),
            pltpu.VMEM((groups * span, planes * depth), jnp.bfloat16),
            pltpu.VMEM((groups * span, cells // 2), jnp.float32),
            pltpu.VMEM((2, nz, groups, fac * NT_DEV, cells // 2), jnp.bfloat16),
            dma((nz,)),
            dma((nz,)),
            dma((nz,)),
            dma((nz,)),
            dma((nz,)),
            dma((nz,)),
            dma((nz,)),
            dma((nz,)),
            dma((pairs, nz)),
            dma((pairs, nz)),
            dma((pairs, nz)),
            dma((pairs, nz)),
            dma((pairs, nz)),
            dma((pairs, nz)),
            dma((nz, 2)),
            dma((nz, 2)),
            dma((nz + 2,)),
            dma,
        ],
        compiler_params=pltpu.CompilerParams(
            collective_id=0, has_side_effects=True, vmem_limit_bytes=60 * 1024 * 1024
        ),
    )(
        neighbours.T,
        counts,
        vis,
        delays.reshape(fac, pairs, 2, blk, lanes),
        tile_of,
        plane_of,
        kernels.reshape(planes * depth, cells),
    )
    spread = out.reshape(nz * groups, fac, NT_DEV, cells).astype(jnp.float32)
    return jnp.transpose(spread, (2, 1, 0, 3))


def solution(mesh):
    return jax.shard_map(
        local,
        mesh=mesh,
        in_specs=(
            P(None, None, None, ("facet", "chan"), None),
            P(),
            P("facet", None, None),
            P("facet", None),
            P("facet", None),
            P("facet"),
            P(),
        ),
        out_specs=P("chan", "facet", None, None),
        check_vma=False,
    )
```

time: 38 us -> 37.8 us (level)
  Pallas kernels: 33.4 us -> 35.9 us
  local copies, waits for them, and re-layouts: 3.65 us -> 1.71 us
  other arithmetic: 0.77 us -> 0 us
    pallas_call x1, Pallas kernels: 33.4 us -> 35.9 us  [local(): pl.pallas_call(functools.partial(kernel, cfg), out_shape=jax.ShapeDtypeSt...]
    unnamed x1 -> x0, local copies, waits for them, and re-layouts: 1.35 us -> none
    select_n x1 -> x0, other arithmetic: 0.77 us -> none  [local(): code = jnp.where(block_id < counts[:, None], plane_of * tiles + tile_of, -1)]
    reshape x1 -> x0, local copies, waits for them, and re-layouts: 0.59 us -> none  [local(): code = code.reshape(fac, 1, blocks)]
where the time goes in v1:
time: 37.8 us; the launch traced here: 37.6 us
  Pallas kernels  35.9 us (95%)
  local copies, waits for them, and re-layouts  1.71 us (5%)
    pallas_call x1, Pallas kernels, local(): pl.pallas_call(functools.partial(kernel, cfg), out_shape=jax.ShapeDtypeSt...  35.9 us
    transpose x1, local copies, waits for them, and re-layouts, local(): return jnp.transpose(spread, (2, 1, 0, 3))  1.71 us

profile of v1, /device:TPU:0, one launch (start us, length us, event | category | flops | bytes accessed | tf_op | source)
XLA Modules:
  0.0 37.6 jit_solution(17164409063591452826)
XLA Ops:
  0.0 35.9 %shard_map.73 = bf16[4,1,32,512]{3,2,1,0:T(8,128)(2,1)} custom-call(s32[4,8]{1,0:T(4,128)} %bitcast.13, s32[2]{0:T(128)} %count_ref.1, bf16[2,8,4,2,32,128]{5,4,3,2,1,0:T(8,128)(2,1)} %bitcast.10, f32[2,4,2,32,128]{4,3,2,1,0:T(8,128)} %bitcast.12, s32[2,256]{1,0:T(2,128)} %tile_ref.1, s32[2,256]{1,0:T(2,128)} %plane_ref.1, bf16[8192,512]{1,0:T(8,128)(2,1)} %bitcast.9), custom_call_target="tpu_custom_call" | custom-call | tf_op jit(solution)/shard_map/pallas_call | solution.py:402
  35.9 1.7 %copy.10 = f32[4,2,16,512]{3,0,1,2:T(4,128)} copy(bf16[4,2,16,512]{3,2,1,0:T(8,128)(2,1)} %bitcast.11) | data formatting | bytes 393216 | tf_op jit(solution)/shard_map/transpose | solution.py:452

commit v2 on v1

--- a/solution.py
+++ b/solution.py
@@ -13,6 +13,8 @@
 NT_DEV = 16
 EDGE = 4
 LANES = 128
+JOINED = 3
+ORDER = (3, 0, 1, 2)
 MESH = pl.DeviceIdType.MESH
 
 
@@ -61,6 +63,7 @@
     pair,
     part,
     got,
+    raw,
     wide,
     rough,
     turns,
@@ -80,6 +83,8 @@
     code_recv,
     part_send,
     part_recv,
+    raw_send,
+    raw_recv,
     row_send,
     row_recv,
     relay_send,
@@ -89,7 +94,7 @@
     own_sem,
     kern_sem,
 ):
-    n, nz, facets, fac, blk, groups, planes, tiles = cfg
+    n, nz, facets, fac, blk, groups, planes, tiles, joined, order = cfg
     me = lax.axis_index("chan")
     zme = lax.axis_index("facet")
     channels = groups * AVG * nz
@@ -112,6 +117,12 @@
     )
 
     def own_copy(c):
+        if c >= joined:
+            return pltpu.make_async_copy(
+                vis_ref.at[:, group_of(c), my_pair, parity],
+                raw.at[me, :, group_of(c)],
+                own_sem.at[c],
+            )
         return pltpu.make_async_copy(
             vis_ref.at[:, group_of(c), :, parity],
             pair.at[parity, :, group_of(c)],
@@ -176,12 +187,27 @@
     def code_copy(d, slot):
         return facet_copy(codes.at[zme], codes, slot, d, code_send, code_recv)
 
-    for c in range(nz):
+    def raw_copy(c, d, slot):
+        peer = lax.rem(me + d, n)
+        return pltpu.make_async_remote_copy(
+            src_ref=vis_ref.at[:, group_of(c), peer // 2, lax.rem(peer, 2)],
+            dst_ref=raw.at[slot, :, group_of(c)],
+            send_sem=raw_send.at[d, c],
+            recv_sem=raw_recv.at[d, c],
+            device_id={"chan": peer},
+            device_id_type=MESH,
+        )
+
+    for c in range(joined):
         mate_copy(c, parity).start()
-    for d in range(1, nz):
-        turn_copy(d, zme).start()
-    for d in range(1, nz):
-        rough_copy(d, zme).start()
+    for c in order:
+        if 0 < c < joined:
+            rough_copy(c, zme).start()
+        if c:
+            turn_copy(c, zme).start()
+        if c >= joined:
+            for d in range(1, n):
+                raw_copy(c, d, me).start()
     for d in range(1, nz):
         code_copy(d, zme).start()
 
@@ -215,6 +241,8 @@
         return lax.rem(my_pair + pairs - d, pairs)
 
     def join_pair(c):
+        if c >= joined:
+            return
         own_copy(c).wait()
         mate_copy(c, 1 - parity).wait_recv()
         if c:
@@ -224,9 +252,8 @@
             slot = i // pairs
             q = lax.rem(i, pairs)
             f = chunk_z[c] * fac + slot
-            cosine, sine = turn_parts(
-                rough[chunk_z[c], slot, q].astype(jnp.float32) * (0.5 / channels)
-            )
+            delay = rough[chunk_z[c], slot, q].astype(jnp.float32) if c else wide[slot, q]
+            cosine, sine = turn_parts(delay * (0.5 / channels))
             real = pair[1, 0, f, q].astype(jnp.float32)
             imag = pair[1, 1, f, q].astype(jnp.float32)
             part[q, 0, f] = (
@@ -247,26 +274,34 @@
             turn_copy(c, chunk_z[c]).wait_recv()
         else:
             own_turns.wait()
-        for d in range(1, pairs):
-            part_copy(c, d, after(d), before(d)).wait_recv()
+        if c < joined:
+            for d in range(1, pairs):
+                part_copy(c, d, after(d), before(d)).wait_recv()
+            source, terms = got, half_avg
+        else:
+            own_copy(c).wait()
+            for d in range(1, n):
+                raw_copy(c, d, lax.rem(me + n - d, n)).wait_recv()
+            source, terms = raw, AVG
+        step_turns = 0.5 * AVG / (terms * channels)
 
         def one(i, carry):
             f = chunk_z[c] * fac + i
             delay = turns[chunk_z[c], i]
-            step_cos, step_sin = turn_parts(delay * (1.0 / channels))
+            step_cos, step_sin = turn_parts(delay * step_turns)
             for g in range(groups):
                 first = (zme * groups + g) * AVG
                 start_cos, start_sin = turn_parts(
                     delay * (1.0 + (0.5 / channels) * first.astype(jnp.float32))
                 )
-                top = (g + 1) * half_avg - 1
-                real = got[top, 0, f].astype(jnp.float32)
-                imag = got[top, 1, f].astype(jnp.float32)
-                for k in range(top - 1, g * half_avg - 1, -1):
-                    next_real = got[k, 0, f].astype(jnp.float32) + (
+                top = (g + 1) * terms - 1
+                real = source[top, 0, f].astype(jnp.float32)
+                imag = source[top, 1, f].astype(jnp.float32)
+                for k in range(top - 1, g * terms - 1, -1):
+                    next_real = source[k, 0, f].astype(jnp.float32) + (
                         real * step_cos - imag * step_sin
                     )
-                    imag = got[k, 1, f].astype(jnp.float32) + (
+                    imag = source[k, 1, f].astype(jnp.float32) + (
                         real * step_sin + imag * step_cos
                     )
                     real = next_real
@@ -317,7 +352,7 @@
     for step in range(nz + len(stages) - 1):
         for lag, stage in enumerate(stages):
             if 0 <= step - lag < nz:
-                stage(step - lag)
+                stage(order[step - lag])
 
     span = facets * NT_DEV
     row_id = lax.broadcasted_iota(jnp.int32, (NT_DEV, span), 0)
@@ -366,15 +401,21 @@
         out_ref[zme, :, :, half * tile : (half + 1) * tile] = final[half, zme]
 
     for c in range(nz):
-        mate_copy(c, parity).wait_send()
+        if c < joined:
+            mate_copy(c, parity).wait_send()
+            for d in range(1, pairs):
+                part_copy(c, d, after(d), my_pair).wait_send()
+        else:
+            for d in range(1, n):
+                raw_copy(c, d, me).wait_send()
         for q in range(pairs):
             row_copy(me, mate, c, row_send.at[q, c], row_recv.at[q, c]).wait_send()
         for q in range(1, pairs):
-            part_copy(c, q, after(q), my_pair).wait_send()
             row_copy(me, mate, c, relay_send.at[q, c], relay_recv.at[q, c]).wait_send()
     for d in range(1, nz):
         turn_copy(d, zme).wait_send()
-        rough_copy(d, zme).wait_send()
+        if d < joined:
+            rough_copy(d, zme).wait_send()
         code_copy(d, zme).wait_send()
     for half in range(2):
         for d in range(1, nz):
@@ -393,7 +434,9 @@
     groups = n * ch_dev // AVG
     tiles = NT_DEV * n
     vis = visibilities.reshape(halves, facets, pairs, 2, blk, lanes)
-    cfg = (n, nz, facets, fac, blk, groups, planes, tiles)
+    joined = min(JOINED, nz)
+    order = ORDER if nz == len(ORDER) else tuple(range(nz))
+    cfg = (n, nz, facets, fac, blk, groups, planes, tiles, joined, order)
     dma = pltpu.SemaphoreType.DMA
     span = facets * NT_DEV
     smem = pl.BlockSpec(memory_space=pltpu.SMEM)
@@ -408,6 +451,7 @@
             pltpu.VMEM((2, halves, facets, pairs, blk, lanes), jnp.bfloat16),
             pltpu.VMEM((pairs, halves, facets, blk, lanes), jnp.bfloat16),
             pltpu.VMEM((pairs, halves, facets, blk, lanes), jnp.bfloat16),
+            pltpu.VMEM((n, halves, facets, blk, lanes), jnp.bfloat16),
             pltpu.VMEM((fac, pairs, blk, lanes), jnp.float32),
             pltpu.VMEM((nz, fac, pairs, blk, lanes), jnp.bfloat16),
             pltpu.VMEM((nz, fac, blk, lanes), jnp.float32),
@@ -427,6 +471,8 @@
             dma((nz,)),
             dma((pairs, nz)),
             dma((pairs, nz)),
+            dma((n, nz)),
+            dma((n, nz)),
             dma((pairs, nz)),
             dma((pairs, nz)),
             dma((pairs, nz)),

time: 37.8 us -> 36 us (0.952)
  Pallas kernels: 35.9 us -> 34.1 us
    pallas_call x1, Pallas kernels: 35.9 us -> 34.1 us  [local(): pl.pallas_call(functools.partial(kernel, cfg), out_shape=jax.ShapeDtypeSt...]
where the time goes in v2:
time: 36 us; the launch traced here: 35.8 us
  Pallas kernels  34.1 us (95%)
  local copies, waits for them, and re-layouts  1.71 us (5%)
    pallas_call x1, Pallas kernels, local(): pl.pallas_call(functools.partial(kernel, cfg), out_shape=jax.ShapeDtypeSt...  34.1 us
    transpose x1, local copies, waits for them, and re-layouts, local(): return jnp.transpose(spread, (2, 1, 0, 3))  1.71 us

profile of v2, /device:TPU:0, one launch (start us, length us, event | category | flops | bytes accessed | tf_op | source)
XLA Modules:
  0.0 35.8 jit_solution(561680089365606636)
XLA Ops:
  0.0 34.1 %shard_map.73 = bf16[4,1,32,512]{3,2,1,0:T(8,128)(2,1)} custom-call(s32[4,8]{1,0:T(4,128)} %bitcast.13, s32[2]{0:T(128)} %count_ref.1, bf16[2,8,4,2,32,128]{5,4,3,2,1,0:T(8,128)(2,1)} %bitcast.10, f32[2,4,2,32,128]{4,3,2,1,0:T(8,128)} %bitcast.12, s32[2,256]{1,0:T(2,128)} %tile_ref.1, s32[2,256]{1,0:T(2,128)} %plane_ref.1, bf16[8192,512]{1,0:T(8,128)(2,1)} %bitcast.9), custom_call_target="tpu_custom_call" | custom-call | tf_op jit(solution)/shard_map/pallas_call | solution.py:445
  34.1 1.7 %copy.10 = f32[4,2,16,512]{3,0,1,2:T(4,128)} copy(bf16[4,2,16,512]{3,2,1,0:T(8,128)(2,1)} %bitcast.11) | data formatting | bytes 393216 | tf_op jit(solution)/shard_map/transpose | solution.py:498

commit v3 on v2

--- a/solution.py
+++ b/solution.py
@@ -330,15 +330,17 @@
     def gather_rows(c):
         if c:
             code_copy(c, chunk_z[c]).wait_recv()
+        tables = [
+            (codes[chunk_z[c], i : i + 1] == wanted).astype(jnp.float32).astype(jnp.bfloat16)
+            for i in range(fac)
+        ]
         row_copy(mate, mate, c, row_send.at[0, c], row_recv.at[0, c]).wait_recv()
         for q in range(1, pairs):
             owner = 2 * before(q) + 1 - parity
             row_copy(owner, mate, c, relay_send.at[q, c], relay_recv.at[q, c]).wait_recv()
         for i in range(fac):
             f = chunk_z[c] * fac + i
-            code = codes[chunk_z[c], i : i + 1]
-            table = (code == wanted).astype(jnp.float32).astype(jnp.bfloat16)
-            summed = jnp.dot(table, rows[f], preferred_element_type=jnp.float32).astype(
+            summed = jnp.dot(tables[i], rows[f], preferred_element_type=jnp.float32).astype(
                 jnp.bfloat16
             )
             for g in range(groups):
@@ -347,12 +349,6 @@
                     lhs[at, 2 * LANES * p : 2 * LANES * (p + 1)] = summed[
                         p * NT_DEV : (p + 1) * NT_DEV, 2 * LANES * g : 2 * LANES * (g + 1)
                     ]
-
-    stages = (join_pair, rotate, relay, gather_rows)
-    for step in range(nz + len(stages) - 1):
-        for lag, stage in enumerate(stages):
-            if 0 <= step - lag < nz:
-                stage(order[step - lag])
 
     span = facets * NT_DEV
     row_id = lax.broadcasted_iota(jnp.int32, (NT_DEV, span), 0)
@@ -367,6 +363,12 @@
         weights.append(weight)
     mix = jnp.concatenate(weights, axis=0).astype(jnp.bfloat16)
     keep = lax.broadcasted_iota(jnp.int32, (span, LANES), 1) >= LANES - edge
+
+    stages = (join_pair, rotate, relay, gather_rows)
+    for step in range(nz + len(stages) - 1):
+        for lag, stage in enumerate(stages):
+            if 0 <= step - lag < nz:
+                stage(order[step - lag])
 
     def fin_copy(half, d, slot):
         return pltpu.make_async_remote_copy(

time: 36 us -> 36 us (level)
  no operation moved by 1% of the time
where the time goes in v3:
time: 36 us; the launch traced here: 35.8 us
  Pallas kernels  34.1 us (95%)
  local copies, waits for them, and re-layouts  1.71 us (5%)
    pallas_call x1, Pallas kernels, local(): pl.pallas_call(functools.partial(kernel, cfg), out_shape=jax.ShapeDtypeSt...  34.1 us
    transpose x1, local copies, waits for them, and re-layouts, local(): return jnp.transpose(spread, (2, 1, 0, 3))  1.71 us

profile of v3, /device:TPU:0, one launch (start us, length us, event | category | flops | bytes accessed | tf_op | source)
XLA Modules:
  0.0 35.8 jit_solution(2999898345877717425)
XLA Ops:
  0.0 34.1 %shard_map.73 = bf16[4,1,32,512]{3,2,1,0:T(8,128)(2,1)} custom-call(s32[4,8]{1,0:T(4,128)} %bitcast.13, s32[2]{0:T(128)} %count_ref.1, bf16[2,8,4,2,32,128]{5,4,3,2,1,0:T(8,128)(2,1)} %bitcast.10, f32[2,4,2,32,128]{4,3,2,1,0:T(8,128)} %bitcast.12, s32[2,256]{1,0:T(2,128)} %tile_ref.1, s32[2,256]{1,0:T(2,128)} %plane_ref.1, bf16[8192,512]{1,0:T(8,128)(2,1)} %bitcast.9), custom_call_target="tpu_custom_call" | custom-call | tf_op jit(solution)/shard_map/pallas_call | solution.py:447
  34.1 1.7 %copy.10 = f32[4,2,16,512]{3,0,1,2:T(4,128)} copy(bf16[4,2,16,512]{3,2,1,0:T(8,128)(2,1)} %bitcast.11) | data formatting | bytes 393216 | tf_op jit(solution)/shard_map/transpose | solution.py:500
